TPU v7x, 32 devices: a whole 2x2x4 slice. The times are simulated.
32 devices in a mesh: seq: 8 (over z, y), head: 4 (over x, core).
Axes of the slice: x: 2, y: 2, z: 4, core: 2. Of those that a mesh axis runs over, the one named last changes fastest.
Arguments:
- queries: bfloat16 [1024, 24576], P('seq', 'head'), may hold values from -325 to 325
- latents: bfloat16 [1024, 576], P('seq'), may hold values from -5 to 5
- doc_ids: int32 [1024], P('seq'), may hold values from 0 to 3, never falling along the last dimension, each value on 1 to 512 neighbouring positions
- key_weight: bfloat16 [512, 16384], P(None, 'head'), may hold values from -0.25 to 0.25
- value_weight: bfloat16 [512, 16384], P(None, 'head'), may hold values from -0.25 to 0.25
- out_grad: bfloat16 [1024, 16384], P('seq', 'head'), may hold values from -6 to 6
Outputs:
- attended: bfloat16 [1024, 16384], P('seq', 'head')
- latent_grad: float32 [1024, 576], P('seq')
- key_weight_grad: float32 [512, 16384], P('seq', 'head')
- value_weight_grad: float32 [512, 16384], P('seq', 'head')
Inputs may be any that keep to these rules, and one draw needn't show every extreme that they name: `doc_ids`: ids never fall along the sequence; every document holds 1 to 512 tokens, and one holds exactly that many.
All inputs are finite; a program needn't handle non-finite values.
Results may differ from a plain program's by a relative error of at most 0.028.
Values may be sent and summed in bfloat16 or wider, within the bound.
A program may use at most 128 MiB of HBM per device.

v0:
```python
import math

import jax
import jax.numpy as jnp
from jax import lax
from jax.sharding import PartitionSpec as P

NOPE = 128
ROPE = 64
VDIM = 128
LATENT = 512
REACH = 4


def shifted(shard, axis, by):
    devices = lax.axis_size(axis)
    pairs = [(i, i + by) for i in range(devices) if 0 <= i + by < devices]
    return lax.ppermute(shard, axis, pairs)


def attend(
    query_block, grad_block, key_nope, value_up, key_rope, key_ids, key_pos, query_ids, query_pos
):
    query_rows = query_block.shape[0]
    key_rows = key_nope.shape[0]
    head_count = key_nope.shape[1] // NOPE
    score_scale = 1.0 / math.sqrt(NOPE + ROPE)
    query_heads = query_block.reshape(query_rows, head_count, NOPE + ROPE)
    grad_heads = grad_block.reshape(query_rows, head_count, VDIM)
    key_heads = key_nope.reshape(key_rows, head_count, NOPE)
    value_heads = value_up.reshape(key_rows, head_count, VDIM)
    scores = jnp.einsum(
        "phd,thd->hpt", query_heads[:, :, :NOPE], key_heads, preferred_element_type=jnp.float32
    )
    scores = scores + jnp.einsum(
        "phr,tr->hpt", query_heads[:, :, NOPE:], key_rope, preferred_element_type=jnp.float32
    )
    scores = scores * score_scale
    visible = (
        (key_pos[None, :] <= query_pos[:, None])
        & (key_pos[None, :] >= 0)
        & (key_ids[None, :] == query_ids[:, None])
    )
    scores = jnp.where(visible[None], scores, -jnp.inf)
    row_top = jnp.max(scores, axis=-1, keepdims=True)
    row_lse = row_top + jnp.log(jnp.sum(jnp.exp(scores - row_top), axis=-1, keepdims=True))
    weight_f = jnp.exp(scores - row_lse)
    weight_b = weight_f.astype(jnp.bfloat16)
    output = jnp.einsum(
        "hpt,thd->phd", weight_b, value_heads, preferred_element_type=jnp.float32
    ).astype(jnp.bfloat16)
    d_weight = jnp.einsum(
        "phd,thd->hpt", grad_heads, value_heads, preferred_element_type=jnp.float32
    )
    row_delta = jnp.sum(grad_heads.astype(jnp.float32) * output.astype(jnp.float32), axis=-1)
    d_score = (weight_f * (d_weight - jnp.transpose(row_delta)[:, :, None]) * score_scale).astype(
        jnp.bfloat16
    )
    d_key = jnp.einsum(
        "hpt,phd->thd", d_score, query_heads, preferred_element_type=jnp.float32
    ).astype(jnp.bfloat16)
    d_value = jnp.einsum(
        "hpt,phd->thd", weight_b, grad_heads, preferred_element_type=jnp.float32
    ).astype(jnp.bfloat16)
    key_grads = jnp.concatenate(
        [
            d_key[:, :, :NOPE].reshape(key_rows, head_count * NOPE),
            d_value.reshape(key_rows, head_count * VDIM),
        ],
        axis=1,
    )
    rope_grads = d_key[:, :, NOPE:].reshape(key_rows, head_count * ROPE)
    return (output.reshape(query_rows, head_count * VDIM), key_grads, rope_grads)


def fetch_blocks(main_part, rope_part, id_part):
    gathered = [(main_part, rope_part, id_part)]
    moving = (main_part, rope_part, id_part)
    for distance in range(1, REACH + 1):
        moving = shifted((moving[0], moving[1], moving[2]), "seq", 1)
        gathered.append(moving)
    ordered = gathered[::-1]
    stacked_main = jnp.concatenate([entry[0] for entry in ordered], axis=0)
    stacked_rope = jnp.concatenate([entry[1] for entry in ordered], axis=0)
    stacked_ids = jnp.concatenate([entry[2] for entry in ordered], axis=0)
    return (stacked_main, stacked_rope, stacked_ids)


def per_device(queries, latents, doc_ids, key_weight, value_weight, out_grad):
    tok_rows = latents.shape[0]
    head_count = key_weight.shape[1] // NOPE
    nope_cols = head_count * NOPE
    seq_index = lax.axis_index("seq")
    weight_both = jnp.concatenate([key_weight, value_weight], axis=1)
    query_pos = seq_index * tok_rows + jnp.arange(tok_rows, dtype=jnp.int32)
    own_latent = latents[:, :LATENT]
    own_rope = latents[:, LATENT:]
    stacked_main, stacked_rope, key_ids = fetch_blocks(own_latent, own_rope, doc_ids)
    upward = jnp.dot(stacked_main, weight_both, preferred_element_type=jnp.float32).astype(
        jnp.bfloat16
    )
    key_nope = upward[:, :nope_cols]
    value_up = upward[:, nope_cols:]
    key_rows = stacked_main.shape[0]
    key_pos = (seq_index - REACH) * tok_rows + jnp.arange(key_rows, dtype=jnp.int32)
    attended, key_grads, rope_grads = attend(
        queries, out_grad, key_nope, value_up, stacked_rope, key_ids, key_pos, doc_ids, query_pos
    )
    own_start = REACH * tok_rows
    latent_term = jnp.einsum(
        "tc,lc->tl", key_grads, weight_both, preferred_element_type=jnp.float32
    )
    rope_term = jnp.sum(rope_grads.astype(jnp.float32).reshape(key_rows, head_count, ROPE), axis=1)
    partial_grad = jnp.concatenate([latent_term, rope_term], axis=1)
    own_grad = partial_grad[own_start:]
    for distance in range(1, REACH + 1):
        slice_start = (REACH - distance) * tok_rows
        own_grad = own_grad + shifted(
            partial_grad[slice_start : slice_start + tok_rows].astype(jnp.bfloat16),
            "seq",
            -distance,
        ).astype(jnp.float32)
    weight_grad = lax.psum_scatter(
        jnp.einsum("tl,tc->lc", stacked_main, key_grads, preferred_element_type=jnp.float32),
        "seq",
        scatter_dimension=0,
        tiled=True,
    )
    latent_grad = lax.psum(own_grad, "head")
    return (attended, latent_grad, weight_grad[:, :nope_cols], weight_grad[:, nope_cols:])


def solution(mesh):
    in_specs = (
        P("seq", "head"),
        P("seq", None),
        P("seq"),
        P(None, "head"),
        P(None, "head"),
        P("seq", "head"),
    )
    out_specs = (P("seq", "head"), P("seq", None), P("seq", "head"), P("seq", "head"))
    return jax.shard_map(
        per_device, mesh=mesh, in_specs=in_specs, out_specs=out_specs, check_vma=False
    )
```

profile of v0, /device:TPU:0, one launch (start us, length us, event | category | flops | bytes accessed | tf_op | source)
XLA Modules:
  0.0 480.8 jit_solution(16549838476198115949)
XLA Ops:
  8.1 5.2 %collective-permute-start.4 = (s32[128]{0:T(128)}, s32[128]{0:T(128)S(1)}, u32[]{:S(2)}, u32[]{:S(2)}) collective-permute-start(s32[128]{0:T(128)} %param.8), channel_id=1, source_target_pairs={{0,4},{4,8},{8,12},{12,16},{16,20},{20,24},{24,28},{1,5},{5,9},{9,... | collective-permute-start | bytes 1544 | tf_op jit(solution)/shard_map/ppermute | solution.py:18
  14.6 4.0 collective-permute-start.8
  25.5 3.3 copy-done.6
  28.8 3.4 collective-permute-start.5
  33.5 4.7 collective-permute-start.6
  38.9 4.8 collective-permute-start.7
  50.4 4.7 collective-permute-start.9
  56.8 4.2 collective-permute-start.10
  62.4 4.7 collective-permute-start.11
  68.2 5.1 %collective-permute-start.1 = (bf16[128,512]{0,1:T(8,128)(2,1)S(1)}, bf16[128,512]{0,1:T(8,128)(2,1)S(1)}, u32[]{:S(2)}, u32[]{:S(2)}) collective-permute-start(bf16[128,512]{0,1:T(8,128)(2,1)S(1)} %collective-permute-done), channel_id=1, source_target_pairs={{0,4},{4,8},{8,12},{12,16},{16,20},{20,24},{24,28},{1,5},{5,9},{9,... | collective-permute-start | bytes 393224 | tf_op jit(solution)/shard_map/ppermute | solution.py:18
  75.8 4.3 collective-permute-start.2
  82.6 4.5 collective-permute-start.3
  89.7 10.7 %convolution_convert_fusion = bf16[640,8192]{1,0:T(8,128)(2,1)} fusion(bf16[640,512]{0,1:T(8,128)(2,1)S(1)} %constant_dynamic-update-slice_fusion, bf16[512,8192]{1,0:T(8,128)(2,1)} %copy-done.6), kind=kOutput, calls=%fused_computation | convolution fusion | flops 5373952000 | bytes 19529728 | tf_op jit(solution)/shard_map/dot_general | solution.py:99
  100.4 12.4 %slice_bitcast_fusion = (bf16[80,32,8,128]{3,2,1,0:T(8,128)(2,1)}, bf16[80,32,8,128]{3,2,1,0:T(8,128)(2,1)}) fusion(bf16[640,8192]{1,0:T(8,128)(2,1)} %convolution_convert_fusion), kind=kLoop, calls=%fused_computation.21 | loop fusion | bytes 20971520
  112.8 3.4 fusion.8
  120.0 3.6 slice-done
  124.5 5.4 %multiply_reduce_fusion = (f32[128,32]{0,1:T(8,128)S(1)}, bf16[32,128,128]{2,1,0:T(8,128)(2,1)}) fusion(bf16[128,4096]{0,1:T(8,128)(2,1)} %copy.24, f32[32,128,640]{1,2,0:T(8,128)S(1)} %get-tuple-element.21, f32[32,128]{1,0:T(8,128)S(1)} %log_add_fusion, bf16[80,32,8,128]{3,2,1,0:T(8,128)(2,1)S(1)} %bitcast.62), kind=kOutput, calls=%fused_computation.30 | convolution fusion | flops 678948864 | bytes 17858560 | tf_op jit(solution)/shard_map/hpt,thd->phd/dot_general | solution.py:49
  129.9 8.7 %convolution_convert_fusion.1 = bf16[32,640,128]{1,2,0:T(8,128)(2,1)} fusion(bf16[128,32,128]{0,2,1:T(8,128)(2,1)} %bitcast.63, f32[32,128,640]{1,2,0:T(8,128)} %copy-done, f32[32,128]{1,0:T(8,128)S(1)} %log_add_fusion), kind=kOutput, calls=%fused_computation.29 | convolution fusion | flops 678952960 | bytes 16793600 | tf_op jit(solution)/shard_map/hpt,phd->thd/dot_general | solution.py:62
  138.6 10.2 %convert_bitcast_fusion = bf16[640,32,192]{0,2,1:T(8,128)(2,1)} fusion(bf16[128,32,192]{0,2,1:T(8,128)(2,1)S(1)} %bitcast.67, f32[32,128,640]{1,2,0:T(8,128)} %copy-done, f32[32,128]{1,0:T(8,128)S(1)} %bitcast.73, f32[32,128]{1,0:T(8,128)S(1)} %log_add_fusion, bf16[128,32,128]{0,2,1:T(8,128)(2,1)S(1)} %bitcast.64, ...), kind=kOutput, calls=%fused_computation.11 | convolution fusion | flops 1694760960 | bytes 26247168 | tf_op jit(solution)/shard_map/hpt,phd->thd/dot_general | solution.py:59
  148.8 5.6 %slice.68 = bf16[640,32,128]{0,2,1:T(8,128)(2,1)} slice(bf16[640,32,192]{0,2,1:T(8,128)(2,1)} %convert_bitcast_fusion), slice={[0:640], [0:32], [0:128]} | slice | bytes 10485760 | tf_op jit(solution)/shard_map/slice | solution.py:67
  154.4 16.5 %fusion.5 = f32[512,8192]{1,0:T(8,128)} fusion(bf16[640,512]{0,1:T(8,128)(2,1)S(1)} %copy-done.11, bf16[640,4096]{0,1:T(8,128)(2,1)} %bitcast.68, bf16[640,4096]{0,1:T(8,128)(2,1)} %bitcast.70), kind=kOutput, calls=%fused_computation.12 | convolution fusion | flops 5389680640 | bytes 27918336 | tf_op jit(solution)/shard_map/tl,tc->lc/dot_general | solution.py:124
  173.1 16.0 %fusion.6 = f32[640,512]{0,1:T(8,128)S(1)} fusion(bf16[512,8192]{1,0:T(8,128)(2,1)} %copy-done.6, bf16[640,4096]{0,1:T(8,128)(2,1)} %bitcast.69, bf16[640,4096]{0,1:T(8,128)(2,1)} %bitcast.71), kind=kOutput, calls=%fused_computation.13 | convolution fusion | flops 5389680640 | bytes 20185088 | tf_op jit(solution)/shard_map/tc,lc->tl/dot_general | solution.py:110
  197.8 25.9 %collective-permute-done.15 = bf16[128,576]{0,1:T(8,128)(2,1)S(1)} collective-permute-done((bf16[128,576]{0,1:T(8,128)(2,1)S(1)}, bf16[128,576]{0,1:T(8,128)(2,1)S(1)}, u32[]{:S(2)}, u32[]{:S(2)}) %collective-permute-start.15) | collective-permute-done | bytes 147488 | tf_op jit(solution)/shard_map/ppermute | solution.py:18
  224.5 244.1 %reduce-scatter.2.cloned.1.call-done = f32[64,8192]{1,0:T(8,128)} async-done(((f32[512,8192]{1,0:T(8,128)}), f32[64,8192]{1,0:T(8,128)}) %reduce-scatter.2.cloned.1.call-update) | async-done | bytes 2097168 | tf_op jit(solution)/shard_map/reduce_scatter | solution.py:123
  (92 shorter events, 49.5 us)
Async XLA Ops:
  8.0 460.6 %reduce-scatter.2.cloned.1.call-start = ((), (), s32[]{:S(2)}) async-start(), calls=%async_computation.2 | async-start | bytes 18874368 | tf_op jit(solution)/shard_map/reduce_scatter | solution.py:123
  8.0 16.9 %copy-start.5 = (bf16[512,4096]{1,0:T(8,128)(2,1)S(1)}, bf16[512,4096]{1,0:T(8,128)(2,1)}, u32[]{:S(2)}) copy-start(bf16[512,4096]{1,0:T(8,128)(2,1)} %param.10) | copy-start | bytes 12582916
  8.1 20.7 %collective-permute-start.4 = (s32[128]{0:T(128)}, s32[128]{0:T(128)S(1)}, u32[]{:S(2)}, u32[]{:S(2)}) collective-permute-start(s32[128]{0:T(128)} %param.8), channel_id=1, source_target_pairs={{0,4},{4,8},{8,12},{12,16},{16,20},{20,24},{24,28},{1,5},{5,9},{9,... | collective-permute-start | bytes 1544 | tf_op jit(solution)/shard_map/ppermute | solution.py:18
  14.6 35.9 %collective-permute-start.8 = (bf16[128,64]{0,1:T(8,128)(2,1)}, bf16[128,64]{0,1:T(8,128)(2,1)}, u32[]{:S(2)}, u32[]{:S(2)}) collective-permute-start(bf16[128,64]{0,1:T(8,128)(2,1)} %slice.53), channel_id=1, source_target_pairs={{0,4},{4,8},{8,12},{12,16},{16,20},{20,24},{24,28},{1,5},{5,9},{9,... | collective-permute-start | bytes 49160 | tf_op jit(solution)/shard_map/ppermute | solution.py:18
  19.5 24.8 %copy-start.8 = (bf16[128,4096]{1,0:T(8,128)(2,1)S(1)}, bf16[128,4096]{1,0:T(8,128)(2,1)}, u32[]{:S(2)}) copy-start(bf16[128,4096]{1,0:T(8,128)(2,1)} %param.11) | copy-start | bytes 3145732
  19.5 26.1 %copy-start.7 = (bf16[128,6144]{1,0:T(8,128)(2,1)S(1)}, bf16[128,6144]{1,0:T(8,128)(2,1)}, u32[]{:S(2)}) copy-start(bf16[128,6144]{1,0:T(8,128)(2,1)} %param.6) | copy-start | bytes 4718596
  19.5 48.6 %collective-permute-start = (bf16[128,512]{0,1:T(8,128)(2,1)S(1)}, bf16[128,512]{0,1:T(8,128)(2,1)S(1)}, u32[]{:S(2)}, u32[]{:S(2)}) collective-permute-start(bf16[128,512]{0,1:T(8,128)(2,1)S(1)} %slice.49), channel_id=1, source_target_pairs={{0,4},{4,8},{8,12},{12,16},{16,20},{20,24},{24,28},{1,5},{5,9},{9,... | collective-permute-start | bytes 393224 | tf_op jit(solution)/shard_map/ppermute | solution.py:18
  25.0 62.2 %copy-start.9 = (bf16[128,576]{0,1:T(8,128)(2,1)S(1)}, bf16[128,576]{0,1:T(8,128)(2,1)}, u32[]{:S(2)}) copy-start(bf16[128,576]{0,1:T(8,128)(2,1)} %param.7) | copy-start | bytes 442372
  28.8 4.7 collective-permute-start.5
  33.5 5.5 %collective-permute-start.6 = (s32[128]{0:T(128)S(1)}, s32[128]{0:T(128)}, u32[]{:S(2)}, u32[]{:S(2)}) collective-permute-start(s32[128]{0:T(128)S(1)} %collective-permute-done.5), channel_id=1, source_target_pairs={{0,4},{4,8},{8,12},{12,16},{16,20},{20,24},{24,28},{1,5},{5,9},{9,... | collective-permute-start | bytes 1544 | tf_op jit(solution)/shard_map/ppermute | solution.py:18
  38.9 7.6 %collective-permute-start.7 = (s32[128]{0:T(128)}, s32[128]{0:T(128)}, u32[]{:S(2)}, u32[]{:S(2)}) collective-permute-start(s32[128]{0:T(128)} %collective-permute-done.6), channel_id=1, source_target_pairs={{0,4},{4,8},{8,12},{12,16},{16,20},{20,24},{24,28},{1,5},{5,9},{9,... | collective-permute-start | bytes 1544 | tf_op jit(solution)/shard_map/ppermute | solution.py:18
  46.5 69.7 %copy-start.2 = (bf16[128,6144]{0,1:T(8,128)(2,1)}, bf16[128,6144]{0,1:T(8,128)(2,1)S(1)}, u32[]{:S(2)}) copy-start(bf16[128,6144]{0,1:T(8,128)(2,1)S(1)} %copy.19) | copy-start | bytes 4718596
  50.4 6.3 %collective-permute-start.9 = (bf16[128,64]{0,1:T(8,128)(2,1)}, bf16[128,64]{0,1:T(8,128)(2,1)S(1)}, u32[]{:S(2)}, u32[]{:S(2)}) collective-permute-start(bf16[128,64]{0,1:T(8,128)(2,1)} %collective-permute-done.8), channel_id=1, source_target_pairs={{0,4},{4,8},{8,12},{12,16},{16,20},{20,24},{24,28},{1,5},{5,9},{9,... | collective-permute-start | bytes 49160 | tf_op jit(solution)/shard_map/ppermute | solution.py:18
  56.8 5.6 %collective-permute-start.10 = (bf16[128,64]{0,1:T(8,128)(2,1)S(1)}, bf16[128,64]{0,1:T(8,128)(2,1)S(1)}, u32[]{:S(2)}, u32[]{:S(2)}) collective-permute-start(bf16[128,64]{0,1:T(8,128)(2,1)S(1)} %collective-permute-done.9), channel_id=1, source_target_pairs={{0,4},{4,8},{8,12},{12,16},{16,20},{20,24},{24,28},{1,5},{5,9},{9,... | collective-permute-start | bytes 49160 | tf_op jit(solution)/shard_map/ppermute | solution.py:18
  62.4 10.9 %collective-permute-start.11 = (bf16[128,64]{0,1:T(8,128)(2,1)S(1)}, bf16[128,64]{0,1:T(8,128)(2,1)S(1)}, u32[]{:S(2)}, u32[]{:S(2)}) collective-permute-start(bf16[128,64]{0,1:T(8,128)(2,1)S(1)} %collective-permute-done.10), channel_id=1, source_target_pairs={{0,4},{4,8},{8,12},{12,16},{16,20},{20,24},{24,28},{1,5},{5,9},{9,... | collective-permute-start | bytes 49160 | tf_op jit(solution)/shard_map/ppermute | solution.py:18
  68.2 7.6 %collective-permute-start.1 = (bf16[128,512]{0,1:T(8,128)(2,1)S(1)}, bf16[128,512]{0,1:T(8,128)(2,1)S(1)}, u32[]{:S(2)}, u32[]{:S(2)}) collective-permute-start(bf16[128,512]{0,1:T(8,128)(2,1)S(1)} %collective-permute-done), channel_id=1, source_target_pairs={{0,4},{4,8},{8,12},{12,16},{16,20},{20,24},{24,28},{1,5},{5,9},{9,... | collective-permute-start | bytes 393224 | tf_op jit(solution)/shard_map/ppermute | solution.py:18
  75.8 6.8 %collective-permute-start.2 = (bf16[128,512]{0,1:T(8,128)(2,1)S(1)}, bf16[128,512]{0,1:T(8,128)(2,1)S(1)}, u32[]{:S(2)}, u32[]{:S(2)}) collective-permute-start(bf16[128,512]{0,1:T(8,128)(2,1)S(1)} %collective-permute-done.1), channel_id=1, source_target_pairs={{0,4},{4,8},{8,12},{12,16},{16,20},{20,24},{24,28},{1,5},{5,9},{9,... | collective-permute-start | bytes 393224 | tf_op jit(solution)/shard_map/ppermute | solution.py:18
  82.6 6.8 %collective-permute-start.3 = (bf16[128,512]{0,1:T(8,128)(2,1)S(1)}, bf16[128,512]{0,1:T(8,128)(2,1)S(1)}, u32[]{:S(2)}, u32[]{:S(2)}) collective-permute-start(bf16[128,512]{0,1:T(8,128)(2,1)S(1)} %collective-permute-done.2), channel_id=1, source_target_pairs={{0,4},{4,8},{8,12},{12,16},{16,20},{20,24},{24,28},{1,5},{5,9},{9,... | collective-permute-start | bytes 393224 | tf_op jit(solution)/shard_map/ppermute | solution.py:18
  171.0 300.7 %all-reduce.2.cloned.1.call-start = ((), (), s32[]{:S(2)}) async-start(), calls=%async_computation.1 | async-start | bytes 589824 | tf_op jit(solution)/shard_map/psum | solution.py:129
  173.1 22.0 %copy-start.4 = (bf16[32,128,128]{2,1,0:T(8,128)(2,1)S(1)}, bf16[32,128,128]{2,1,0:T(8,128)(2,1)}, u32[]{:S(2)}) copy-start(bf16[32,128,128]{2,1,0:T(8,128)(2,1)} %get-tuple-element.23) | copy-start | bytes 3145732
  190.0 7.8 %collective-permute-start.12 = (bf16[128,576]{0,1:T(8,128)(2,1)}, bf16[128,576]{0,1:T(8,128)(2,1)S(1)}, u32[]{:S(2)}, u32[]{:S(2)}) collective-permute-start(bf16[128,576]{0,1:T(8,128)(2,1)} %get-tuple-element.16), channel_id=1, source_target_pairs={{4,0},{8,4},{12,8},{16,12},{20,16},{24,20},{28,24},{5,1},{9,5},{13... | collective-permute-start | bytes 442376 | tf_op jit(solution)/shard_map/ppermute | solution.py:18
  191.3 32.4 %collective-permute-start.15 = (bf16[128,576]{0,1:T(8,128)(2,1)S(1)}, bf16[128,576]{0,1:T(8,128)(2,1)S(1)}, u32[]{:S(2)}, u32[]{:S(2)}) collective-permute-start(bf16[128,576]{0,1:T(8,128)(2,1)S(1)} %get-tuple-element.17), channel_id=1, source_target_pairs={{16,0},{20,4},{24,8},{28,12},{17,1},{21,5},{25,9},{29,13},{18,2},{... | collective-permute-start | bytes 442376 | tf_op jit(solution)/shard_map/ppermute | solution.py:18
  192.6 31.1 %collective-permute-start.14 = (bf16[128,576]{0,1:T(8,128)(2,1)S(1)}, bf16[128,576]{0,1:T(8,128)(2,1)S(1)}, u32[]{:S(2)}, u32[]{:S(2)}) collective-permute-start(bf16[128,576]{0,1:T(8,128)(2,1)S(1)} %get-tuple-element.18), channel_id=1, source_target_pairs={{12,0},{16,4},{20,8},{24,12},{28,16},{13,1},{17,5},{21,9},{25,13},... | collective-permute-start | bytes 442376 | tf_op jit(solution)/shard_map/ppermute | solution.py:18
  193.9 29.8 %collective-permute-start.13 = (bf16[128,576]{0,1:T(8,128)(2,1)S(1)}, bf16[128,576]{0,1:T(8,128)(2,1)S(1)}, u32[]{:S(2)}, u32[]{:S(2)}) collective-permute-start(bf16[128,576]{0,1:T(8,128)(2,1)S(1)} %get-tuple-element.19), channel_id=1, source_target_pairs={{8,0},{12,4},{16,8},{20,12},{24,16},{28,20},{9,1},{13,5},{17,9},{2... | collective-permute-start | bytes 442376 | tf_op jit(solution)/shard_map/ppermute | solution.py:18
  (10 other events, 86.6 us)
Sparse Core Ops, SparseCore 0:
  171.1 297.4 reduce-scatter.1
Sparse Core Ops, SparseCore 1:
  224.6 51.4 all-reduce.1
where the time goes:
time: 482 us; the launch traced here: 481 us
  waiting for transfers between devices  279 us (58%)
  matrix products  72.8 us (15%)
  starting transfers between devices  57.9 us (12%)
  local copies, waits for them, and re-layouts  47.5 us (10%)
  between operations  15.9 us (3%)
  other arithmetic  7.48 us (2%)
    reduce_scatter x1, waiting for transfers between devices, per_device(): lax.psum_scatter(jnp.einsum('tl,tc->lc', stacked_main, key_grads, preferr...  244 us
    ppermute x16, starting transfers between devices, shifted(): return lax.ppermute(shard, axis, pairs)  57.8 us
    ppermute x16, waiting for transfers between devices, shifted(): return lax.ppermute(shard, axis, pairs)  35.1 us
    unnamed x50, local copies, waits for them, and re-layouts  34 us
    dot_general x1, matrix products, per_device(): jnp.einsum('tl,tc->lc', stacked_main, key_grads, preferred_element_type=j...  16.5 us
    dot_general x1, matrix products, per_device(): jnp.einsum('tc,lc->tl', key_grads, weight_both, preferred_element_type=jn...  16 us
    dot_general x1, matrix products, per_device(): jnp.dot(stacked_main, weight_both, preferred_element_type=jnp.float32)  10.7 us
    dot_general x1, matrix products, attend(): jnp.einsum('hpt,phd->thd', d_score, query_heads, preferred_element_type=j...  10.2 us
  transfers between devices with their start and end apart: 18, of which 10 were waited for; matrix products, arithmetic and copies ran while one was open for 9% of the time, Pallas kernels for 0%

commit v1 on v0

v1 whole, which is shorter than its diff:
```python
import functools
import math

import jax
import jax.numpy as jnp
from jax import lax
from jax.experimental import pallas as pl
from jax.experimental.pallas import tpu as pltpu
from jax.sharding import PartitionSpec as P

NOPE = 128
ROPE = 64
VDIM = 128
LATENT = 512
REACH = 4
PAIR = 2
Y_LAG = 2
Z_LAG = 2
MESH = pl.DeviceIdType.MESH
F32 = jnp.float32
BF16 = jnp.bfloat16


def dot(a, b, ca, cb):
    return lax.dot_general(a, b, (((ca,), (cb,)), ((), ())), preferred_element_type=F32)


def kernel(
    n, hn, steps, grid_steps,
    latx_ref, qid_ref, q_ref, g_ref, kw_ref, vw_ref,
    att_ref, lg_ref, kwg_ref, vwg_ref,
    lat_all, lat_t, bias, lgacc, part, ry, rzp, rzm, ls, lr, hb,
    lat_ss, lat_rs, y_ss, y_rs, z_ss, zp_rs, zm_rs, l_ss, l_rs, h_ss, h_rs,
):
    j = pl.program_id(0)
    s = lax.axis_index("seq")
    h = lax.axis_index("head")
    line = n // 2
    z, y = s // 2, s % 2
    tok = latx_ref.shape[0]
    keys = (REACH + 1) * tok
    scale = 1.0 / math.sqrt(NOPE + ROPE)

    def lat_copy(d):
        return pltpu.make_async_remote_copy(
            src_ref=latx_ref,
            dst_ref=lat_all.at[pl.ds((REACH - d) * tok, tok)],
            send_sem=lat_ss.at[d - 1], recv_sem=lat_rs.at[d - 1],
            device_id=(s + d, h), device_id_type=MESH,
        )

    def y_copy(i):
        return pltpu.make_async_remote_copy(
            src_ref=part.at[i, 1 - y], dst_ref=ry.at[i],
            send_sem=y_ss.at[i], recv_sem=y_rs.at[i],
            device_id=(s + 1 - 2 * y, h), device_id_type=MESH,
        )

    def z_copy(i, d, up):
        return pltpu.make_async_remote_copy(
            src_ref=part.at[i, y, d], dst_ref=(rzp if up else rzm).at[i, d],
            send_sem=z_ss.at[i, d], recv_sem=(zp_rs if up else zm_rs).at[i, d],
            device_id=(s + 2 if up else s - 2, h), device_id_type=MESH,
        )

    def l_copy(d):
        return pltpu.make_async_remote_copy(
            src_ref=ls.at[d - 1], dst_ref=lr.at[d - 1],
            send_sem=l_ss.at[d - 1], recv_sem=l_rs.at[d - 1],
            device_id=(s - d, h), device_id_type=MESH,
        )

    def h_copy(k, slot):
        return pltpu.make_async_remote_copy(
            src_ref=hb.at[slot], dst_ref=hb.at[slot],
            send_sem=h_ss.at[k - 1], recv_sem=h_rs.at[slot],
            device_id=(s, (h + k) % hn), device_id_type=MESH,
        )

    @pl.when(j == 0)
    def _():
        barrier = pltpu.get_barrier_semaphore()
        for d in range(1, REACH + 1):
            @pl.when(s + d < n)
            def _():
                pl.semaphore_signal(barrier, inc=1, device_id=(s + d, h), device_id_type=MESH)

            @pl.when(s - d >= 0)
            def _():
                pl.semaphore_signal(barrier, inc=1, device_id=(s - d, h), device_id_type=MESH)
        for k in range(1, hn):
            pl.semaphore_signal(barrier, inc=1, device_id=(s, (h + k) % hn), device_id_type=MESH)
        pl.semaphore_wait(barrier, jnp.minimum(s, REACH) + jnp.minimum(n - 1 - s, REACH) + hn - 1)
        for d in range(1, REACH + 1):
            @pl.when(s + d < n)
            def _():
                lat_copy(d).start()
        lat_all[REACH * tok:, :] = latx_ref[...]
        lgacc[...] = jnp.zeros_like(lgacc)
        for d in range(1, REACH + 1):
            @pl.when(s - d >= 0)
            def _():
                lat_copy(d).wait_recv()

            @pl.when(s - d < 0)
            def _():
                lat_all[(REACH - d) * tok:(REACH - d + 1) * tok, :] = jnp.zeros((tok, latx_ref.shape[1]), BF16)
        for d in range(1, REACH + 1):
            @pl.when(s + d < n)
            def _():
                lat_copy(d).wait_send()
        lat_t[...] = jnp.transpose(lat_all[:, :LATENT])
        key_row = lax.broadcasted_iota(jnp.int32, (keys, tok), 0)
        query_row = lax.broadcasted_iota(jnp.int32, (keys, tok), 1) + REACH * tok
        key_id = lat_all[:, LATENT + ROPE:LATENT + ROPE + 1].astype(F32)
        visible = (
            (key_row <= query_row)
            & (key_row >= (REACH - s) * tok)
            & (key_id == qid_ref[...])
        )
        bias[...] = jnp.where(visible, 0.0, -jnp.inf)

    @pl.when(j < steps)
    def _():
        lat = lat_all[:, :LATENT]
        rope = lat_all[:, LATENT:LATENT + ROPE]
        kw, vw = kw_ref[...], vw_ref[...]
        k2 = dot(lat, kw, 1, 0).astype(BF16)
        v2 = dot(lat, vw, 1, 0).astype(BF16)
        dks, dvs, rope_sum = [], [], None
        for a in range(PAIR):
            q = q_ref[:, a * (NOPE + ROPE):(a + 1) * (NOPE + ROPE)]
            g = g_ref[:, a * VDIM:(a + 1) * VDIM]
            v = v2[:, a * VDIM:(a + 1) * VDIM]
            k = jnp.concatenate([k2[:, a * NOPE:(a + 1) * NOPE], rope], axis=1)
            sc = dot(k, q, 1, 1) * scale + bias[...]
            e = jnp.exp(sc - jnp.max(sc, axis=0, keepdims=True))
            p = e * (1.0 / jnp.sum(e, axis=0, keepdims=True))
            pb = p.astype(BF16)
            att_ref[:, a * VDIM:(a + 1) * VDIM] = dot(pb, v, 0, 0).astype(BF16)
            dp = dot(v, g, 1, 1)
            delta = jnp.sum(pb.astype(F32) * dp, axis=0, keepdims=True)
            ds = (p * (dp - delta) * scale).astype(BF16)
            dk = dot(ds, q, 1, 0).astype(BF16)
            dvs.append(dot(pb, g, 1, 0).astype(BF16))
            dks.append(dk[:, :NOPE])
            r = dk[:, NOPE:].astype(F32)
            rope_sum = r if rope_sum is None else rope_sum + r
        dk2 = jnp.concatenate(dks, axis=1)
        dv2 = jnp.concatenate(dvs, axis=1)
        lgacc[:, :LATENT] += dot(dk2, kw, 1, 1) + dot(dv2, vw, 1, 1)
        lgacc[:, LATENT:] += rope_sum
        lt = lat_t[...]
        rows = part.shape[3]
        for col, dd in ((0, dk2), (PAIR * NOPE, dv2)):
            wg = dot(lt, dd, 1, 0).astype(BF16).reshape(line, 2, rows, dd.shape[1])
            for yy in range(2):
                part[j, yy, :, :, col:col + dd.shape[1]] = wg[:, yy]
        y_copy(j).start()

    @pl.when(j == steps - 1)
    def _():
        for d in range(1, REACH + 1):
            ls[d - 1] = lgacc[(REACH - d) * tok:(REACH - d + 1) * tok, :].astype(BF16)
        for d in range(1, REACH + 1):
            @pl.when(s - d >= 0)
            def _():
                l_copy(d).start()

    @pl.when(j == steps + 1)
    def _():
        for d in range(1, REACH + 1):
            @pl.when(s + d < n)
            def _():
                l_copy(d).wait_recv()
                lgacc[REACH * tok:, :] += lr[d - 1].astype(F32)
        hb[h] = lgacc[REACH * tok:, :].astype(BF16)
        for k in range(1, hn):
            h_copy(k, h).start()

    @pl.when(j == steps + 3)
    def _():
        for k in range(1, hn):
            h_copy(k, (h + k) % hn).wait_recv()
        total = hb[0].astype(F32)
        for k in range(1, hn):
            total = total + hb[k].astype(F32)
        lg_ref[...] = total

    iy = j - Y_LAG

    @pl.when((iy >= 0) & (iy < steps))
    def _():
        y_copy(iy).wait_recv()
        part[iy, y] = (part[iy, y].astype(F32) + ry[iy].astype(F32)).astype(BF16)

    for up in (True, False):
        pos = z if up else line - 1 - z
        iz = j - Y_LAG - Z_LAG * pos
        buf = rzp if up else rzm

        @pl.when((iz >= 0) & (iz < steps))
        def _():
            for dist in range(1, line):
                d = z + dist if up else z - dist

                @pl.when((d < line) & (d >= 0))
                def _():
                    @pl.when(pos > 0)
                    def _():
                        z_copy(iz, d, up).wait_recv()
                        part[iz, y, d] = (part[iz, y, d].astype(F32) + buf[iz, d].astype(F32)).astype(BF16)
                    z_copy(iz, d, up).start()

    fin = j - Y_LAG - Z_LAG * (line - 1)

    @pl.when((fin >= 0) & (fin < steps))
    def _():
        half = PAIR * NOPE
        own = part[fin, y, z].astype(F32)
        kwg_ref[...] = own[:, :half]
        vwg_ref[...] = own[:, half:]
        for up in (True, False):
            buf = rzp if up else rzm

            @pl.when(z > 0 if up else z < line - 1)
            def _():
                z_copy(fin, z, up).wait_recv()
                got = buf[fin, z].astype(F32)
                kwg_ref[...] += got[:, :half]
                vwg_ref[...] += got[:, half:]

    @pl.when(j == grid_steps - 1)
    def _():
        for d in range(1, REACH + 1):
            @pl.when(s - d >= 0)
            def _():
                l_copy(d).wait_send()
        for k in range(1, hn):
            h_copy(k, h).wait_send()

        def drain(i, c):
            y_copy(i).wait_send()
            for d in range(line):
                @pl.when(d != z)
                def _():
                    z_copy(i, d, True).wait_send()
            return c

        lax.fori_loop(0, steps, drain, 0)


def per_device(n, hn, queries, latents, doc_ids, key_weight, value_weight, out_grad):
    tok = latents.shape[0]
    heads = key_weight.shape[1] // NOPE
    steps = heads // PAIR
    line = n // 2
    rows = LATENT // n
    lag = Y_LAG + Z_LAG * (line - 1)
    grid_steps = steps + max(lag, 4)
    keys = (REACH + 1) * tok
    width = LATENT + ROPE
    latx = jnp.concatenate(
        [latents, jnp.broadcast_to(doc_ids.astype(BF16)[:, None], (tok, 64))], axis=1
    )
    qid = doc_ids.astype(F32)[None, :]
    whole = pl.BlockSpec(memory_space=pltpu.VMEM)

    def at(lag_by):
        return lambda j: (0, jnp.clip(j - lag_by, 0, steps - 1))

    dma = pltpu.SemaphoreType.DMA
    att, lg, kwg, vwg = pl.pallas_call(
        functools.partial(kernel, n, hn, steps, grid_steps),
        grid=(grid_steps,),
        out_shape=(
            jax.ShapeDtypeStruct((tok, heads * VDIM), BF16),
            jax.ShapeDtypeStruct((tok, width), F32),
            jax.ShapeDtypeStruct((rows, heads * NOPE), F32),
            jax.ShapeDtypeStruct((rows, heads * VDIM), F32),
        ),
        in_specs=[
            whole,
            whole,
            pl.BlockSpec((tok, PAIR * (NOPE + ROPE)), at(0)),
            pl.BlockSpec((tok, PAIR * VDIM), at(0)),
            pl.BlockSpec((LATENT, PAIR * NOPE), at(0)),
            pl.BlockSpec((LATENT, PAIR * VDIM), at(0)),
        ],
        out_specs=(
            pl.BlockSpec((tok, PAIR * VDIM), at(0)),
            whole,
            pl.BlockSpec((rows, PAIR * NOPE), at(lag)),
            pl.BlockSpec((rows, PAIR * VDIM), at(lag)),
        ),
        scratch_shapes=[
            pltpu.VMEM((keys, latx.shape[1]), BF16),
            pltpu.VMEM((LATENT, keys), BF16),
            pltpu.VMEM((keys, tok), F32),
            pltpu.VMEM((keys, width), F32),
            pltpu.VMEM((steps, 2, line, rows, PAIR * (NOPE + VDIM)), BF16),
            pltpu.VMEM((steps, line, rows, PAIR * (NOPE + VDIM)), BF16),
            pltpu.VMEM((steps, line, rows, PAIR * (NOPE + VDIM)), BF16),
            pltpu.VMEM((steps, line, rows, PAIR * (NOPE + VDIM)), BF16),
            pltpu.VMEM((REACH, tok, width), BF16),
            pltpu.VMEM((REACH, tok, width), BF16),
            pltpu.VMEM((hn, tok, width), BF16),
            dma((REACH,)), dma((REACH,)),
            dma((steps,)), dma((steps,)),
            dma((steps, line)), dma((steps, line)), dma((steps, line)),
            dma((REACH,)), dma((REACH,)),
            dma((max(hn - 1, 1),)), dma((hn,)),
        ],
        compiler_params=pltpu.CompilerParams(
            collective_id=0,
            has_side_effects=True,
            dimension_semantics=("arbitrary",),
            vmem_limit_bytes=60 * 1024 * 1024,
        ),
    )(latx, qid, queries, out_grad, key_weight, value_weight)
    return att, lg, kwg, vwg


def solution(mesh):
    in_specs = (
        P("seq", "head"),
        P("seq", None),
        P("seq"),
        P(None, "head"),
        P(None, "head"),
        P("seq", "head"),
    )
    out_specs = (P("seq", "head"), P("seq", None), P("seq", "head"), P("seq", "head"))
    body = functools.partial(per_device, mesh.shape["seq"], mesh.shape["head"])
    return jax.shard_map(
        body, mesh=mesh, in_specs=in_specs, out_specs=out_specs, check_vma=False
    )
```

time: 482 us -> 160 us (0.33)
  waiting for transfers between devices: 279 us -> 0 us
  Pallas kernels: 0 us -> 149 us
  matrix products: 72.8 us -> 0 us
  starting transfers between devices: 57.9 us -> 0 us
  local copies, waits for them, and re-layouts: 47.5 us -> 8.6 us
  between operations: 15.9 us -> 0.66 us
  other arithmetic: 7.48 us -> 2 us
    reduce_scatter x1 -> x0, waiting for transfers between devices: 244 us -> none  [per_device(): lax.psum_scatter(jnp.einsum('tl,tc->lc', stacked_main, key_grads, preferr...]
    pallas_call x0 -> x1, Pallas kernels: none -> 149 us  [per_device(): pl.pallas_call(functools.partial(kernel, n, hn, steps, grid_steps), grid=...]
    dot_general x8 -> x0, matrix products: 72.8 us -> none  [the longest x1 16.5 us: per_device(): jnp.einsum('tl,tc->lc', stacked_main, key_grads, preferred_element_type=j...]
    ppermute x16 -> x0, starting transfers between devices: 57.8 us -> none  [shifted(): return lax.ppermute(shard, axis, pairs)]
    ppermute x16 -> x0, waiting for transfers between devices: 35.1 us -> none  [shifted(): return lax.ppermute(shard, axis, pairs)]
    unnamed x50 -> x6, local copies, waits for them, and re-layouts: 34 us -> 6.59 us
    slice x5 -> x0, local copies, waits for them, and re-layouts: 11.7 us -> none  [the longest x1 5.64 us: attend(): d_key[:, :, :NOPE].reshape(key_rows, head_count * NOPE)]
  transfers between devices with their start and end apart: 18 -> 0, of which waited for: 10 -> 0; matrix products, arithmetic and copies ran while one was open for 9% -> 0% of each run, Pallas kernels for 0% -> 0%
where the time goes in v1:
time: 160 us
  Pallas kernels  149 us (93%)
  local copies, waits for them, and re-layouts  8.6 us (5%)
  other arithmetic  2 us (1%)
    pallas_call x1, Pallas kernels, per_device(): pl.pallas_call(functools.partial(kernel, n, hn, steps, grid_steps), grid=...  149 us
    unnamed x6, local copies, waits for them, and re-layouts  6.59 us

profile of v1, /device:TPU:0, one launch (start us, length us, event | category | flops | bytes accessed | tf_op | source)
XLA Modules:
  0.0 160.1 jit_solution(12577302009529059762)
XLA Ops:
  0.6 1.2 convert_bitcast_fusion
  1.9 0.1 broadcast_in_dim.4
  2.0 1.1 copy.10
  3.0 0.8 pad_maximum_fusion.latx_ref
  3.8 148.9 %shard_map.93 = (bf16[128,4096]{1,0:T(8,128)(2,1)}, f32[128,576]{1,0:T(8,128)}, f32[64,4096]{1,0:T(8,128)}, f32[64,4096]{1,0:T(8,128)}) custom-call(bf16[128,640]{1,0:T(8,128)(2,1)} %pad_maximum_fusion.latx_ref, f32[1,128]{1,0:T(1,128)} %get-tuple-element.8.qid_ref, bf16[128,6144]{1,0:T(8,128)(2,1)} %q_ref.1, bf16[128,4096]{1,0:T(8,128)(2,1)} %g_ref.1, ...), custom_call_target="tpu_custom_call" | custom-call | tf_op jit(solution)/shard_map/pallas_call | solution.py:273
  152.6 0.0 copy-start
  152.7 1.9 %copy.11 = f32[128,576]{0,1:T(8,128)} copy(f32[128,576]{1,0:T(8,128)} %get-tuple-element.5) | data formatting | bytes 589824 | tf_op jit(solution)/shard_map/pallas_call | solution.py:273
  154.6 2.3 %copy.15 = bf16[128,4096]{1,0:T(8,128)(2,1)} copy(bf16[128,4096]{1,0:T(8,128)(2,1)} %get-tuple-element.14) | data formatting | bytes 2097152
  156.9 2.3 %copy.16 = f32[64,4096]{1,0:T(8,128)} copy(f32[64,4096]{1,0:T(8,128)} %get-tuple-element.16) | data formatting | bytes 2097152
  159.1 0.0 copy-done
  159.1 1.0 copy.17
Async XLA Ops:
  152.6 6.5 %copy-start = (f32[64,4096]{1,0:T(8,128)S(1)}, f32[64,4096]{1,0:T(8,128)}, u32[]{:S(2)}) copy-start(f32[64,4096]{1,0:T(8,128)} %get-tuple-element.17) | copy-start | bytes 3145732

commit v2 on v1

--- a/solution.py
+++ b/solution.py
@@ -14,8 +14,9 @@
 LATENT = 512
 REACH = 4
 PAIR = 2
-Y_LAG = 2
+Y_LAG = 8
 Z_LAG = 2
+F_LAG = 3
 MESH = pl.DeviceIdType.MESH
 F32 = jnp.float32
 BF16 = jnp.bfloat16
@@ -25,28 +26,48 @@
     return lax.dot_general(a, b, (((ca,), (cb,)), ((), ())), preferred_element_type=F32)
 
 
+def line_first(i, steps):
+    return (i % 4 == 1) & (i < steps // 2)
+
+
 def kernel(
-    n, hn, steps, grid_steps,
-    latx_ref, qid_ref, q_ref, g_ref, kw_ref, vw_ref,
+    n, hn, steps, grid_steps, fin_lag,
+    lat_ref, qid_ref, q_ref, g_ref, kw_ref, vw_ref,
     att_ref, lg_ref, kwg_ref, vwg_ref,
-    lat_all, lat_t, bias, lgacc, part, ry, rzp, rzm, ls, lr, hb,
-    lat_ss, lat_rs, y_ss, y_rs, z_ss, zp_rs, zm_rs, l_ss, l_rs, h_ss, h_rs,
+    latx, lat_all, lat_t, bias, lgacc, part, ry, rzp, rzm, ls, lr, hb,
+    lat_ss, lat_rs, f_ss, f_rs, y_ss, y_rs, z_ss, zp_rs, zm_rs, l_ss, l_rs, h_ss, h_rs,
 ):
     j = pl.program_id(0)
     s = lax.axis_index("seq")
     h = lax.axis_index("head")
     line = n // 2
     z, y = s // 2, s % 2
-    tok = latx_ref.shape[0]
+    tok = lat_ref.shape[0]
+
     keys = (REACH + 1) * tok
     scale = 1.0 / math.sqrt(NOPE + ROPE)
 
     def lat_copy(d):
         return pltpu.make_async_remote_copy(
-            src_ref=latx_ref,
-            dst_ref=lat_all.at[pl.ds((REACH - d) * tok, tok)],
+            src_ref=latx.at[h],
+            dst_ref=lat_all.at[REACH - d, h],
             send_sem=lat_ss.at[d - 1], recv_sem=lat_rs.at[d - 1],
             device_id=(s + d, h), device_id_type=MESH,
+        )
+
+    def f_copy(d, k, slot):
+        return pltpu.make_async_remote_copy(
+            src_ref=lat_all.at[REACH - d, slot],
+            dst_ref=lat_all.at[REACH - d, slot],
+            send_sem=f_ss.at[k - 1, d - 1], recv_sem=f_rs.at[slot, d - 1],
+            device_id=(s, (h + k) % hn), device_id_type=MESH,
+        )
+
+    def y_late_copy(i):
+        return pltpu.make_async_remote_copy(
+            src_ref=part.at[i, 1 - y, z], dst_ref=ry.at[i, 0],
+            send_sem=y_ss.at[i], recv_sem=y_rs.at[i],
+            device_id=(s + 1 - 2 * y, h), device_id_type=MESH,
         )
 
     def y_copy(i):
@@ -56,9 +77,11 @@
             device_id=(s + 1 - 2 * y, h), device_id_type=MESH,
         )
 
-    def z_copy(i, d, up):
-        return pltpu.make_async_remote_copy(
-            src_ref=part.at[i, y, d], dst_ref=(rzp if up else rzm).at[i, d],
+    def z_copy(i, d, up, both):
+        buf = rzp if up else rzm
+        return pltpu.make_async_remote_copy(
+            src_ref=part.at[i, :, d] if both else part.at[i, y, d],
+            dst_ref=buf.at[i, :, d] if both else buf.at[i, y, d],
             send_sem=z_ss.at[i, d], recv_sem=(zp_rs if up else zm_rs).at[i, d],
             device_id=(s + 2 if up else s - 2, h), device_id_type=MESH,
         )
@@ -79,6 +102,9 @@
 
     @pl.when(j == 0)
     def _():
+        ids = jnp.transpose(jnp.broadcast_to(qid_ref[...].astype(F32), (tok, tok)))
+        lx = jnp.concatenate([lat_ref[...], ids[:, :latx.shape[2] - lat_ref.shape[1]].astype(BF16)], axis=1)
+        latx[...] = lx.reshape(latx.shape)
         barrier = pltpu.get_barrier_semaphore()
         for d in range(1, REACH + 1):
             @pl.when(s + d < n)
@@ -95,35 +121,39 @@
             @pl.when(s + d < n)
             def _():
                 lat_copy(d).start()
-        lat_all[REACH * tok:, :] = latx_ref[...]
+        lat_all[REACH] = latx[...]
         lgacc[...] = jnp.zeros_like(lgacc)
         for d in range(1, REACH + 1):
             @pl.when(s - d >= 0)
             def _():
                 lat_copy(d).wait_recv()
+                for k in range(1, hn):
+                    f_copy(d, k, h).start()
 
             @pl.when(s - d < 0)
             def _():
-                lat_all[(REACH - d) * tok:(REACH - d + 1) * tok, :] = jnp.zeros((tok, latx_ref.shape[1]), BF16)
-        for d in range(1, REACH + 1):
-            @pl.when(s + d < n)
-            def _():
-                lat_copy(d).wait_send()
-        lat_t[...] = jnp.transpose(lat_all[:, :LATENT])
+                lat_all[REACH - d] = jnp.zeros(lat_all.shape[1:], BF16)
+        for d in range(1, REACH + 1):
+            @pl.when(s - d >= 0)
+            def _():
+                for k in range(1, hn):
+                    f_copy(d, k, (h + k) % hn).wait_recv()
+        lat_t[...] = jnp.transpose(lat_all[...].reshape(keys, lat_all.shape[3])[:, :LATENT])
         key_row = lax.broadcasted_iota(jnp.int32, (keys, tok), 0)
         query_row = lax.broadcasted_iota(jnp.int32, (keys, tok), 1) + REACH * tok
-        key_id = lat_all[:, LATENT + ROPE:LATENT + ROPE + 1].astype(F32)
+        key_id = lat_all[...].reshape(keys, lat_all.shape[3])[:, LATENT + ROPE:LATENT + ROPE + 1].astype(F32)
         visible = (
             (key_row <= query_row)
             & (key_row >= (REACH - s) * tok)
-            & (key_id == qid_ref[...])
+            & (key_id == qid_ref[...].astype(F32))
         )
         bias[...] = jnp.where(visible, 0.0, -jnp.inf)
 
     @pl.when(j < steps)
     def _():
-        lat = lat_all[:, :LATENT]
-        rope = lat_all[:, LATENT:LATENT + ROPE]
+        lat_rows = lat_all[...].reshape(keys, lat_all.shape[3])
+        lat = lat_rows[:, :LATENT]
+        rope = lat_rows[:, LATENT:LATENT + ROPE]
         kw, vw = kw_ref[...], vw_ref[...]
         k2 = dot(lat, kw, 1, 0).astype(BF16)
         v2 = dot(lat, vw, 1, 0).astype(BF16)
@@ -156,7 +186,9 @@
             wg = dot(lt, dd, 1, 0).astype(BF16).reshape(line, 2, rows, dd.shape[1])
             for yy in range(2):
                 part[j, yy, :, :, col:col + dd.shape[1]] = wg[:, yy]
-        y_copy(j).start()
+        @pl.when(jnp.logical_not(line_first(j, steps)))
+        def _():
+            y_copy(j).start()
 
     @pl.when(j == steps - 1)
     def _():
@@ -189,46 +221,74 @@
 
     iy = j - Y_LAG
 
-    @pl.when((iy >= 0) & (iy < steps))
+    @pl.when((iy >= 0) & (iy < steps) & jnp.logical_not(line_first(iy, steps)))
     def _():
         y_copy(iy).wait_recv()
         part[iy, y] = (part[iy, y].astype(F32) + ry[iy].astype(F32)).astype(BF16)
 
-    for up in (True, False):
-        pos = z if up else line - 1 - z
-        iz = j - Y_LAG - Z_LAG * pos
+    def hop(iz, pos, up, both):
         buf = rzp if up else rzm
-
-        @pl.when((iz >= 0) & (iz < steps))
-        def _():
-            for dist in range(1, line):
-                d = z + dist if up else z - dist
-
-                @pl.when((d < line) & (d >= 0))
+        which = slice(None) if both else y
+        for dist in range(1, line):
+            d = z + dist if up else z - dist
+
+            @pl.when((d < line) & (d >= 0))
+            def _():
+                @pl.when(pos > 0)
                 def _():
-                    @pl.when(pos > 0)
-                    def _():
-                        z_copy(iz, d, up).wait_recv()
-                        part[iz, y, d] = (part[iz, y, d].astype(F32) + buf[iz, d].astype(F32)).astype(BF16)
-                    z_copy(iz, d, up).start()
-
-    fin = j - Y_LAG - Z_LAG * (line - 1)
+                    z_copy(iz, d, up, both).wait_recv()
+                    part[iz, which, d] = (part[iz, which, d].astype(F32) + buf[iz, which, d].astype(F32)).astype(BF16)
+                z_copy(iz, d, up, both).start()
+
+    for both in (True, False):
+        for up in (True, False):
+            pos = z if up else line - 1 - z
+            iz = j - F_LAG * pos if both else j - Y_LAG - Z_LAG * pos
+
+            @pl.when((iz >= 0) & (iz < steps) & (line_first(iz, steps) == both))
+            def _():
+                hop(iz, pos, up, both)
+
+    il = j - F_LAG * (line - 1) - 1
+
+    @pl.when((il >= 0) & (il < steps) & line_first(il, steps))
+    def _():
+        for up in (True, False):
+            buf = rzp if up else rzm
+
+            @pl.when(z > 0 if up else z < line - 1)
+            def _():
+                z_copy(il, z, up, True).wait_recv()
+                part[il, :, z] = (part[il, :, z].astype(F32) + buf[il, :, z].astype(F32)).astype(BF16)
+        y_late_copy(il).start()
+
+    fin = j - fin_lag
+    half = PAIR * NOPE
 
     @pl.when((fin >= 0) & (fin < steps))
     def _():
-        half = PAIR * NOPE
         own = part[fin, y, z].astype(F32)
         kwg_ref[...] = own[:, :half]
         vwg_ref[...] = own[:, half:]
-        for up in (True, False):
-            buf = rzp if up else rzm
-
-            @pl.when(z > 0 if up else z < line - 1)
-            def _():
-                z_copy(fin, z, up).wait_recv()
-                got = buf[fin, z].astype(F32)
-                kwg_ref[...] += got[:, :half]
-                vwg_ref[...] += got[:, half:]
+
+        @pl.when(line_first(fin, steps))
+        def _():
+            y_late_copy(fin).wait_recv()
+            got = ry[fin, 0].astype(F32)
+            kwg_ref[...] += got[:, :half]
+            vwg_ref[...] += got[:, half:]
+
+        @pl.when(jnp.logical_not(line_first(fin, steps)))
+        def _():
+            for up in (True, False):
+                buf = rzp if up else rzm
+
+                @pl.when(z > 0 if up else z < line - 1)
+                def _():
+                    z_copy(fin, z, up, False).wait_recv()
+                    got = buf[fin, y, z].astype(F32)
+                    kwg_ref[...] += got[:, :half]
+                    vwg_ref[...] += got[:, half:]
 
     @pl.when(j == grid_steps - 1)
     def _():
@@ -239,12 +299,25 @@
         for k in range(1, hn):
             h_copy(k, h).wait_send()
 
+        for d in range(1, REACH + 1):
+            @pl.when(s + d < n)
+            def _():
+                lat_copy(d).wait_send()
+
+            @pl.when(s - d >= 0)
+            def _():
+                for k in range(1, hn):
+                    f_copy(d, k, h).wait_send()
+
         def drain(i, c):
-            y_copy(i).wait_send()
-            for d in range(line):
-                @pl.when(d != z)
+            for both in (True, False):
+                @pl.when(line_first(i, steps) == both)
                 def _():
-                    z_copy(i, d, True).wait_send()
+                    (y_late_copy if both else y_copy)(i).wait_send()
+                    for d in range(line):
+                        @pl.when(d != z)
+                        def _():
+                            z_copy(i, d, True, both).wait_send()
             return c
 
         lax.fori_loop(0, steps, drain, 0)
@@ -256,14 +329,12 @@
     steps = heads // PAIR
     line = n // 2
     rows = LATENT // n
-    lag = Y_LAG + Z_LAG * (line - 1)
+    lag = max(Y_LAG + Z_LAG * (line - 1), F_LAG * (line - 1) + 4)
     grid_steps = steps + max(lag, 4)
     keys = (REACH + 1) * tok
     width = LATENT + ROPE
-    latx = jnp.concatenate(
-        [latents, jnp.broadcast_to(doc_ids.astype(BF16)[:, None], (tok, 64))], axis=1
-    )
-    qid = doc_ids.astype(F32)[None, :]
+    ids = doc_ids.reshape(1, tok)
+    wide = width + 64
     whole = pl.BlockSpec(memory_space=pltpu.VMEM)
 
     def at(lag_by):
@@ -271,13 +342,13 @@
 
     dma = pltpu.SemaphoreType.DMA
     att, lg, kwg, vwg = pl.pallas_call(
-        functools.partial(kernel, n, hn, steps, grid_steps),
+        functools.partial(kernel, n, hn, steps, grid_steps, lag),
         grid=(grid_steps,),
         out_shape=(
-            jax.ShapeDtypeStruct((tok, heads * VDIM), BF16),
-            jax.ShapeDtypeStruct((tok, width), F32),
-            jax.ShapeDtypeStruct((rows, heads * NOPE), F32),
-            jax.ShapeDtypeStruct((rows, heads * VDIM), F32),
+            pltpu.HBM((tok, heads * VDIM), BF16),
+            pltpu.HBM((tok, width), F32),
+            pltpu.HBM((rows, heads * NOPE), F32),
+            pltpu.HBM((rows, heads * VDIM), F32),
         ),
         in_specs=[
             whole,
@@ -294,18 +365,20 @@
             pl.BlockSpec((rows, PAIR * VDIM), at(lag)),
         ),
         scratch_shapes=[
-            pltpu.VMEM((keys, latx.shape[1]), BF16),
+            pltpu.VMEM((hn, tok // hn, wide), BF16),
+            pltpu.VMEM((REACH + 1, hn, tok // hn, wide), BF16),
             pltpu.VMEM((LATENT, keys), BF16),
             pltpu.VMEM((keys, tok), F32),
             pltpu.VMEM((keys, width), F32),
             pltpu.VMEM((steps, 2, line, rows, PAIR * (NOPE + VDIM)), BF16),
             pltpu.VMEM((steps, line, rows, PAIR * (NOPE + VDIM)), BF16),
-            pltpu.VMEM((steps, line, rows, PAIR * (NOPE + VDIM)), BF16),
-            pltpu.VMEM((steps, line, rows, PAIR * (NOPE + VDIM)), BF16),
+            pltpu.VMEM((steps, 2, line, rows, PAIR * (NOPE + VDIM)), BF16),
+            pltpu.VMEM((steps, 2, line, rows, PAIR * (NOPE + VDIM)), BF16),
             pltpu.VMEM((REACH, tok, width), BF16),
             pltpu.VMEM((REACH, tok, width), BF16),
             pltpu.VMEM((hn, tok, width), BF16),
             dma((REACH,)), dma((REACH,)),
+            dma((max(hn - 1, 1), REACH)), dma((hn, REACH)),
             dma((steps,)), dma((steps,)),
             dma((steps, line)), dma((steps, line)), dma((steps, line)),
             dma((REACH,)), dma((REACH,)),
@@ -317,7 +390,7 @@
             dimension_semantics=("arbitrary",),
             vmem_limit_bytes=60 * 1024 * 1024,
         ),
-    )(latx, qid, queries, out_grad, key_weight, value_weight)
+    )(latents, ids, queries, out_grad, key_weight, value_weight)
     return att, lg, kwg, vwg
 
 

time: 160 us -> 159 us (level)
  other arithmetic: 2 us -> 0 us
where the time goes in v2:
time: 159 us
  Pallas kernels  149 us (94%)
  local copies, waits for them, and re-layouts  9.17 us (6%)
    pallas_call x1, Pallas kernels, per_device(): pl.pallas_call(functools.partial(kernel, n, hn, steps, grid_steps, lag),...  149 us
    unnamed x6, local copies, waits for them, and re-layouts  7.24 us

profile of v2, /device:TPU:0, one launch (start us, length us, event | category | flops | bytes accessed | tf_op | source)
XLA Modules:
  0.0 159.0 jit_solution(10367154900210228906)
XLA Ops:
  0.6 1.7 %copy.10.lat_ref = bf16[128,576]{1,0:T(8,128)(2,1)} copy(bf16[128,576]{0,1:T(8,128)(2,1)} %param.7) | data formatting | bytes 294912 | tf_op args[1]
  2.3 149.2 %shard_map.93 = (bf16[128,4096]{1,0:T(8,128)(2,1)}, f32[128,576]{1,0:T(8,128)}, f32[64,4096]{1,0:T(8,128)}, f32[64,4096]{1,0:T(8,128)}) custom-call(bf16[128,576]{1,0:T(8,128)(2,1)} %copy.10.lat_ref, s32[1,128]{1,0:T(1,128)} %bitcast.1, bf16[128,6144]{1,0:T(8,128)(2,1)} %q_ref.1, bf16[128,4096]{1,0:T(8,128)(2,1)} %g_ref.1, bf16[512,4096]{1,0:T(8,128)(2,1)} %kw_ref.1, ...), custom_call_target="tpu_custom_call" | custom-call | tf_op jit(solution)/shard_map/pallas_call | solution.py:344
  151.6 0.0 copy-start
  151.6 1.9 %copy.11 = f32[128,576]{0,1:T(8,128)} copy(f32[128,576]{1,0:T(8,128)} %get-tuple-element.5) | data formatting | bytes 589824 | tf_op jit(solution)/shard_map/pallas_call | solution.py:344
  153.5 2.3 %copy.15 = bf16[128,4096]{1,0:T(8,128)(2,1)} copy(bf16[128,4096]{1,0:T(8,128)(2,1)} %get-tuple-element.12) | data formatting | bytes 2097152
  155.8 2.3 %copy.16 = f32[64,4096]{1,0:T(8,128)} copy(f32[64,4096]{1,0:T(8,128)} %get-tuple-element.14) | data formatting | bytes 2097152
  158.1 0.0 copy-done
  158.1 1.0 copy.17
Async XLA Ops:
  151.6 6.5 %copy-start = (f32[64,4096]{1,0:T(8,128)S(1)}, f32[64,4096]{1,0:T(8,128)}, u32[]{:S(2)}) copy-start(f32[64,4096]{1,0:T(8,128)} %get-tuple-element.15) | copy-start | bytes 3145732
